TPU v7x, 32 devices: a whole 2x2x4 slice. The times are simulated.
32 devices in a mesh: frag: 8 (over z, y), blk: 4 (over x, core).
Axes of the slice: x: 2, y: 2, z: 4, core: 2. Of those that a mesh axis runs over, the one named last changes fastest.
Arguments:
- amps: float32 [8, 128, 8, 128], P('frag', 'blk'), may hold values from -1.5 to 1.5
- exch: float32 [8, 128, 8, 128], P('frag', 'blk'), may hold values from -4 to 4
- factors: bfloat16 [8, 384, 128, 128], P('frag', 'blk'), may hold values from -0.109375 to 0.109375
- occupied_pair_ladder: float32 [8, 8, 8], P('frag'), may hold values from -1 to 1
- virtual_fock_block: float32 [8, 128, 128], P('frag'), may hold values from -0.1875 to 0.1875
- virtual_orbital_energy: float32 [8, 128], P('frag'), may hold values from 1 to 3
- pair_energy: float32 [8, 8], P('frag'), may hold values from -1.5 to -0.5
- energy_weight: int32 [8, 8], P('frag'), may hold values from 0 to 2
- export_rows: int32 [8, 2, 2], P('frag'), may hold values from 2 to 5, as said below
Outputs:
- new_amps: float32 [8, 128, 8, 128], P('frag', 'blk')
- res_norms: float32 [8, 2], P('frag')
- energy: float32 [], replicated
Inputs may be any that keep to these rules, and one draw needn't show every extreme that they name: `export_rows`: for each fragment the 4 entries are distinct core rows.
All inputs are finite; a program needn't handle non-finite values.
Results may differ from a plain program's by a relative error of at most 0.0009.
Values may be sent and summed in bfloat16 or wider, within the bound.
A program may use at most 128 MiB of HBM per device.

v0:
```python
import functools

import jax
import jax.numpy as jnp
from jax import lax
from jax.experimental import pallas as pl
from jax.experimental.pallas import tpu as pltpu
from jax.sharding import PartitionSpec as P

PASSES = 2
CHUNK = 2
AUX_BLOCK = 8
MESH = pl.DeviceIdType.MESH
NT = (((1,), (1,)), ((), ()))


def thirds(value):
    high = value.astype(jnp.bfloat16)
    rest = value - high.astype(jnp.float32)
    middle = rest.astype(jnp.bfloat16)
    return high, middle, (rest - middle.astype(jnp.float32)).astype(jnp.bfloat16)


def split_left(value):
    high, middle, small = thirds(value)
    return jnp.concatenate([high, high, middle, high, middle, small], axis=1)


def split_right(value):
    high, middle, small = thirds(value)
    return jnp.concatenate([high, middle, high, small, middle, high], axis=0)


def kernel(
    blocks,
    frags,
    amps_ref,
    exch_ref,
    factors_hbm,
    hole_ref,
    fock_ref,
    orbital_ref,
    pair_ref,
    weight_ref,
    export_ref,
    new_ref,
    norm_ref,
    energy_ref,
    fact,
    amp,
    low,
    low_t,
    half0,
    half1,
    acc,
    acc1,
    part,
    recv,
    base,
    fock_t,
    fock_col,
    row_energy,
    row_t,
    sent_rows,
    got_rows,
    sums,
    frag_sums,
    left_ref,
    right_ref,
    fact_sem,
    ag_send,
    ag_recv,
    rs_send,
    rs_recv,
    ex_send,
    ex_recv,
    sum_send,
    sum_recv,
    fs_send,
    fs_recv,
):
    me = lax.axis_index("blk")
    frag = lax.axis_index("frag")
    _, rows, pairs, virt = amps_ref.shape
    aux = fact.shape[0]
    steps = aux // AUX_BLOCK
    border = export_ref.shape[2]
    peers = [lax.rem(me + j, blocks) for j in range(1, blocks)]
    frag_peers = [lax.rem(frag + j, frags) for j in range(1, frags)]
    chunks = pairs // CHUNK
    starts = sorted(
        range(0, pairs, CHUNK), key=lambda p: p < border or p + CHUNK > pairs - border
    )
    core_chunks = sum(1 for p in starts if border <= p and p + CHUNK <= pairs - border)

    load = pltpu.make_async_copy(factors_hbm.at[0], fact, fact_sem)
    load.start()

    for p in range(pairs):
        value = amps_ref[0, :, p, :]
        amp[0, p] = value
        low[0, me, p] = value.astype(jnp.bfloat16)

    barrier = pltpu.get_barrier_semaphore()
    for peer in peers:
        pl.semaphore_signal(barrier, inc=1, device_id={"blk": peer}, device_id_type=MESH)
    for peer in frag_peers:
        pl.semaphore_signal(barrier, inc=1, device_id={"frag": peer}, device_id_type=MESH)
    pl.semaphore_wait(barrier, blocks - 1 + frags - 1)

    pending = []

    def gather(sweep, start):
        copies = []
        for j, peer in enumerate(peers):
            where = low.at[sweep, me, pl.ds(start, CHUNK)]
            copy = pltpu.make_async_remote_copy(
                src_ref=where,
                dst_ref=where,
                send_sem=ag_send.at[sweep, start // CHUNK, j],
                recv_sem=ag_recv.at[sweep, start // CHUNK, j],
                device_id={"blk": peer},
                device_id_type=MESH,
            )
            copy.start()
            copies.append(copy)
        pending.extend(copies)
        return copies

    def scatter(sweep, start):
        copies = []
        for j, peer in enumerate(peers):
            copy = pltpu.make_async_remote_copy(
                src_ref=part.at[sweep, peer, pl.ds(start, CHUNK)],
                dst_ref=recv.at[sweep, j, pl.ds(start, CHUNK)],
                send_sem=rs_send.at[sweep, start // CHUNK, j],
                recv_sem=rs_recv.at[sweep, start // CHUNK, j],
                device_id={"blk": peer},
                device_id_type=MESH,
            )
            copy.start()
            copies.append(copy)
        pending.extend(copies)
        return copies

    gathers = {(0, start): gather(0, start) for start in starts}

    offset = pl.multiple_of(me * rows, rows)
    fock_t[...] = split_right(fock_ref[0].T)
    column = lax.broadcasted_iota(jnp.int32, (virt, virt), 1)
    own = (column >= offset) & (column < offset + rows)
    fock_col[...] = split_left(jnp.where(own, fock_ref[0], 0.0))
    row_t[...] = jnp.broadcast_to(orbital_ref[...], (virt, virt)).T
    row_energy[...] = row_t[pl.ds(offset, rows), :] + orbital_ref[...]

    def make_base(sweep):
        def product(p, carry):
            right_ref[p] = jnp.dot(
                split_left(amp[sweep, p]), fock_t[...], preferred_element_type=jnp.float32
            )
            return carry

        lax.fori_loop(0, pairs, product, 0)
        for p in range(pairs):
            total = exch_ref[0, :, p, :] + right_ref[p]
            for r in range(pairs):
                total = total + hole_ref[0, p, r] * amp[sweep, r]
            total = total - (row_energy[...] - pair_ref[0, p]) * amp[sweep, p]
            base[sweep, p] = total

    make_base(0)
    load.wait()

    def first_half(index, half):
        at = pl.multiple_of(index * AUX_BLOCK, AUX_BLOCK)
        slab = fact[pl.ds(at, AUX_BLOCK)].reshape(AUX_BLOCK * virt, virt)
        done = lax.dot_general(
            low_t[...], slab, NT, preferred_element_type=jnp.float32
        ).astype(jnp.bfloat16)
        for q in range(AUX_BLOCK):
            for p in range(CHUNK):
                half[q * virt : (q + 1) * virt, p * virt : (p + 1) * virt] = done[
                    p * virt : (p + 1) * virt, q * virt : (q + 1) * virt
                ]

    def second_half(index, half, acc):
        at = pl.multiple_of(index * AUX_BLOCK, AUX_BLOCK)
        slab = jnp.concatenate([fact[at + q] for q in range(AUX_BLOCK)], axis=1)
        acc[...] += jnp.dot(slab, half[...], preferred_element_type=jnp.float32)

    def compute(sweep, start):
        for i in range(CHUNK):
            whole = low[sweep, :, start + i].reshape(virt, virt)
            low_t[i * virt : (i + 1) * virt, :] = whole.T
        acc[...] = jnp.zeros_like(acc)
        acc1[...] = jnp.zeros_like(acc1)
        first_half(0, half0)

        def body(i, carry):
            second_half(2 * i, half0, acc)
            first_half(2 * i + 1, half1)
            second_half(2 * i + 1, half1, acc1)
            first_half(jnp.minimum(2 * i + 2, steps - 1), half0)
            return carry

        lax.fori_loop(0, steps // 2, body, 0)
        def left(i, carry):
            whole = jnp.concatenate([amp[sweep, start + i]] * blocks, axis=0)
            left_ref[i] = jnp.dot(
                fock_col[...], split_right(whole), preferred_element_type=jnp.float32
            )
            return carry

        lax.fori_loop(0, CHUNK, left, 0)
        for i in range(CHUNK):
            cols = slice(i * virt, (i + 1) * virt)
            total = (acc[:, cols] + acc1[:, cols]).T + left_ref[i]
            for k in range(blocks):
                part[sweep, k, start + i] = total[k * rows : (k + 1) * rows]

    norm_sums = [jnp.zeros((8, virt), jnp.float32) for _ in range(PASSES)]

    def finish(sweep, start, copies):
        for copy in copies:
            copy.wait_recv()
        for p in range(start, start + CHUNK):
            residual = base[sweep, p] + part[sweep, me, p]
            for j in range(blocks - 1):
                residual = residual + recv[sweep, j, p]
            norm_sums[sweep] += jnp.sum((residual * residual).reshape(rows // 8, 8, virt), axis=0)
            value = amp[sweep, p] + residual / (row_energy[...] - pair_ref[0, p])
            amp[sweep + 1, p] = value
            if sweep + 1 < PASSES:
                low[sweep + 1, me, p] = value.astype(jnp.bfloat16)
        if sweep + 1 < PASSES:
            gathers[sweep + 1, start] = gather(sweep + 1, start)
        if start == starts[-1] and sweep + 1 < PASSES:
            make_base(sweep + 1)

    exports = []

    def export():
        for side, target in ((0, lax.rem(frag + 1, frags)), (1, lax.rem(frag + frags - 1, frags))):
            for r in range(border):
                sent_rows[side, r] = amp[PASSES, export_ref[0, side, r]]
            copy = pltpu.make_async_remote_copy(
                src_ref=sent_rows.at[side],
                dst_ref=got_rows.at[side],
                send_sem=ex_send.at[side],
                recv_sem=ex_recv.at[side],
                device_id={"frag": target},
                device_id_type=MESH,
            )
            copy.start()
            exports.append(copy)
        pending.extend(exports)

    waiting = None
    finished = 0
    for sweep in range(PASSES):
        for start in starts:
            for copy in gathers[sweep, start]:
                copy.wait_recv()
            compute(sweep, start)
            copies = scatter(sweep, start)
            if waiting is not None:
                finish(*waiting)
                if waiting[0] == PASSES - 1:
                    finished += 1
                    if finished == core_chunks:
                        export()
            waiting = (sweep, start, copies)
    finish(*waiting)

    for copy in exports:
        copy.wait_recv()
    energy = jnp.zeros((8, virt), jnp.float32)
    for p in range(pairs):
        value = amp[PASSES, p]
        if p < border:
            value = jnp.where(frag > 0, got_rows[0, p], value)
        if p >= pairs - border:
            value = jnp.where(frag < frags - 1, got_rows[1, p - (pairs - border)], value)
        new_ref[0, :, p, :] = value
        product = jnp.sum((value * exch_ref[0, :, p, :]).reshape(rows // 8, 8, virt), axis=0)
        energy = energy + (weight_ref[0, p].astype(jnp.float32) * 0.5) * product

    for s in range(PASSES):
        sums[me, s] = norm_sums[s]
    sums[me, PASSES] = energy
    copies = []
    for j, peer in enumerate(peers):
        copy = pltpu.make_async_remote_copy(
            src_ref=sums.at[me],
            dst_ref=sums.at[me],
            send_sem=sum_send.at[j],
            recv_sem=sum_recv.at[j],
            device_id={"blk": peer},
            device_id_type=MESH,
        )
        copy.start()
        copies.append(copy)
    for copy in copies:
        copy.wait_recv()
    pending.extend(copies)
    totals = jnp.sum(sums[...], axis=0)
    frag_sums[frag] = totals[PASSES]
    copies = []
    for j, peer in enumerate(frag_peers):
        copy = pltpu.make_async_remote_copy(
            src_ref=frag_sums.at[frag],
            dst_ref=frag_sums.at[frag],
            send_sem=fs_send.at[j],
            recv_sem=fs_recv.at[j],
            device_id={"frag": peer},
            device_id_type=MESH,
        )
        copy.start()
        copies.append(copy)
    norms = [jnp.sqrt(jnp.sum(jnp.sum(totals[s], axis=0, keepdims=True), axis=1, keepdims=True)) for s in range(PASSES)]
    lane = lax.broadcasted_iota(jnp.int32, (1, PASSES), 1)
    line = jnp.zeros((1, PASSES), jnp.float32)
    for s in range(PASSES):
        line = jnp.where(lane == s, norms[s], line)
    norm_ref[...] = line
    for copy in copies:
        copy.wait_recv()
    pending.extend(copies)
    whole = jnp.sum(frag_sums[...], axis=0)
    energy_ref[...] = -jnp.sum(jnp.sum(whole, axis=0, keepdims=True), axis=1, keepdims=True) / (virt * virt)
    for copy in pending:
        copy.wait_send()


def on_device(blocks, frags, *args):
    amps, _, factors = args[:3]
    _, rows, pairs, virt = amps.shape
    aux = factors.shape[1]
    border = args[-1].shape[2]
    chunks = pairs // CHUNK
    vmem = pl.BlockSpec(memory_space=pltpu.VMEM)
    smem = pl.BlockSpec(memory_space=pltpu.SMEM)
    f32, bf16 = jnp.float32, jnp.bfloat16
    dma = pltpu.SemaphoreType.DMA
    new_amps, norms, energy = pl.pallas_call(
        functools.partial(kernel, blocks, frags),
        out_shape=(
            jax.ShapeDtypeStruct(amps.shape, f32),
            jax.ShapeDtypeStruct((1, PASSES), f32),
            jax.ShapeDtypeStruct((1, 1), f32),
        ),
        in_specs=[
            vmem,
            vmem,
            pl.BlockSpec(memory_space=pl.ANY),
            smem,
            vmem,
            vmem,
            smem,
            smem,
            smem,
        ],
        out_specs=(vmem, vmem, vmem),
        scratch_shapes=[
            pltpu.VMEM((aux, virt, virt), bf16),
            pltpu.VMEM((PASSES + 1, pairs, rows, virt), f32),
            pltpu.VMEM((PASSES, blocks, pairs, rows, virt), bf16),
            pltpu.VMEM((CHUNK * virt, virt), bf16),
            pltpu.VMEM((AUX_BLOCK * virt, CHUNK * virt), bf16),
            pltpu.VMEM((AUX_BLOCK * virt, CHUNK * virt), bf16),
            pltpu.VMEM((virt, CHUNK * virt), f32),
            pltpu.VMEM((virt, CHUNK * virt), f32),
            pltpu.VMEM((PASSES, blocks, pairs, rows, virt), f32),
            pltpu.VMEM((PASSES, blocks - 1, pairs, rows, virt), f32),
            pltpu.VMEM((PASSES, pairs, rows, virt), f32),
            pltpu.VMEM((6 * virt, virt), bf16),
            pltpu.VMEM((virt, 6 * virt), bf16),
            pltpu.VMEM((rows, virt), f32),
            pltpu.VMEM((virt, virt), f32),
            pltpu.VMEM((2, border, rows, virt), f32),
            pltpu.VMEM((2, border, rows, virt), f32),
            pltpu.VMEM((blocks, PASSES + 1, 8, virt), f32),
            pltpu.VMEM((frags, 8, virt), f32),
            pltpu.VMEM((CHUNK, virt, virt), f32),
            pltpu.VMEM((pairs, rows, virt), f32),
            dma,
            dma((PASSES, chunks, blocks - 1)),
            dma((PASSES, chunks, blocks - 1)),
            dma((PASSES, chunks, blocks - 1)),
            dma((PASSES, chunks, blocks - 1)),
            dma((2,)),
            dma((2,)),
            dma((blocks - 1,)),
            dma((blocks - 1,)),
            dma((frags - 1,)),
            dma((frags - 1,)),
        ],
        compiler_params=pltpu.CompilerParams(
            collective_id=0, has_side_effects=True, vmem_limit_bytes=48 * 2**20
        ),
    )(*args)
    return new_amps, norms, energy.reshape(())


def solution(mesh):
    placed = (
        P("frag", "blk", None, None),
        P("frag", "blk", None, None),
        P("frag", "blk", None, None),
        P("frag", None, None),
        P("frag", None, None),
        P("frag", None),
        P("frag", None),
        P("frag", None),
        P("frag", None, None),
    )
    return jax.shard_map(
        functools.partial(on_device, mesh.shape["blk"], mesh.shape["frag"]),
        mesh=mesh,
        in_specs=placed,
        out_specs=(P("frag", "blk", None, None), P("frag", None), P()),
        check_vma=False,
    )
```

profile of v0, /device:TPU:0, one launch (start us, length us, event | category | flops | bytes accessed | tf_op | source)
XLA Modules:
  0.0 73.4 jit_solution(16685947081246574342)
XLA Ops:
  0.6 0.0 copy-start
  0.6 1.9 %copy-done = bf16[1,96,128,128]{3,2,1,0:T(8,128)(2,1)S(1)} copy-done((bf16[1,96,128,128]{3,2,1,0:T(8,128)(2,1)S(1)}, bf16[1,96,128,128]{3,2,1,0:T(8,128)(2,1)}, u32[]{:S(2)}) %copy-start) | copy-done | bytes 3145752
  2.5 0.0 copy-start.1
  2.5 0.9 %copy-done.1 = f32[1,32,8,128]{3,2,1,0:T(8,128)S(1)} copy-done((f32[1,32,8,128]{3,2,1,0:T(8,128)S(1)}, f32[1,32,8,128]{3,2,1,0:T(8,128)}, u32[]{:S(2)}) %copy-start.1) | copy-done | bytes 131096
  3.4 0.0 copy-start.2
  3.4 0.9 %copy-done.2 = f32[1,32,8,128]{3,2,1,0:T(8,128)S(1)} copy-done((f32[1,32,8,128]{3,2,1,0:T(8,128)S(1)}, f32[1,32,8,128]{3,2,1,0:T(8,128)}, u32[]{:S(2)}) %copy-start.2) | copy-done | bytes 131096
  4.3 0.0 copy-start.3
  4.3 0.8 %copy-done.3 = f32[1,128,128]{2,1,0:T(8,128)S(1)} copy-done((f32[1,128,128]{2,1,0:T(8,128)S(1)}, f32[1,128,128]{2,1,0:T(8,128)}, u32[]{:S(2)}) %copy-start.3) | copy-done | bytes 65560
  5.2 0.0 copy-start.4
  5.2 0.7 copy-done.4
  5.9 0.0 copy-start.5
  5.9 0.7 copy-done.5
  6.5 0.0 copy-start.6
  6.5 0.7 copy-done.6
  7.2 0.0 copy-start.7
  7.2 0.7 copy-done.7
  7.9 0.0 copy-start.8
  7.9 0.7 copy-done.8
  8.5 62.0 %shard_map.112 = (f32[1,32,8,128]{3,2,1,0:T(8,128)S(1)}, f32[1,2]{1,0:T(1,128)S(1)}, f32[1,1]{1,0:T(1,128)}) custom-call(f32[1,32,8,128]{3,2,1,0:T(8,128)S(1)} %copy-done.1, f32[1,32,8,128]{3,2,1,0:T(8,128)S(1)} %copy-done.2, bf16[1,96,128,128]{3,2,1,0:T(8,128)(2,1)S(1)} %copy-done, f32[1,8,8]{2,1,0:T(8,128)S(1)} %copy-done.4, f32[1,128,128]{2,1,0:T(8,128)S(1)} %copy-done.3, ...), custom_call_target="tpu_custom_call" | custom-call | tf_op jit(solution)/shard_map/pallas_call | solution.py:345
  70.5 0.7 copy.15
  71.1 0.5 copy.16
Async XLA Ops:
  0.6 1.9 %copy-start = (bf16[1,96,128,128]{3,2,1,0:T(8,128)(2,1)S(1)}, bf16[1,96,128,128]{3,2,1,0:T(8,128)(2,1)}, u32[]{:S(2)}) copy-start(bf16[1,96,128,128]{3,2,1,0:T(8,128)(2,1)} %factors_hbm.1) | copy-start | bytes 9437188
  2.5 0.9 %copy-start.1 = (f32[1,32,8,128]{3,2,1,0:T(8,128)S(1)}, f32[1,32,8,128]{3,2,1,0:T(8,128)}, u32[]{:S(2)}) copy-start(f32[1,32,8,128]{3,2,1,0:T(8,128)} %amps_ref.1) | copy-start | bytes 393220
  3.4 0.9 %copy-start.2 = (f32[1,32,8,128]{3,2,1,0:T(8,128)S(1)}, f32[1,32,8,128]{3,2,1,0:T(8,128)}, u32[]{:S(2)}) copy-start(f32[1,32,8,128]{3,2,1,0:T(8,128)} %exch_ref.1) | copy-start | bytes 393220
  4.3 0.8 %copy-start.3 = (f32[1,128,128]{2,1,0:T(8,128)S(1)}, f32[1,128,128]{2,1,0:T(8,128)}, u32[]{:S(2)}) copy-start(f32[1,128,128]{2,1,0:T(8,128)} %fock_ref.1) | copy-start | bytes 196612
  5.2 0.7 copy-start.4
  5.9 0.7 copy-start.5
  6.5 0.7 copy-start.6
  7.2 0.7 copy-start.7
  7.9 0.7 copy-start.8
where the time goes:
time: 73.7 us; the launch traced here: 73.4 us
  Pallas kernels  62 us (84%)
  local copies, waits for them, and re-layouts  9.03 us (12%)
  between operations  2.41 us (3%)
    pallas_call x1, Pallas kernels, on_device(): pl.pallas_call(functools.partial(kernel, blocks, frags), out_shape=(jax.S...  62 us
    unnamed x20, local copies, waits for them, and re-layouts  9.03 us

commit v1 on v0

v1 whole, which is shorter than its diff:
```python
import functools

import jax
import jax.numpy as jnp
from jax import lax
from jax.experimental import pallas as pl
from jax.experimental.pallas import tpu as pltpu
from jax.sharding import PartitionSpec as P

PASSES = 2
CHUNK = 2
UNITS = 2
GROUP = 8
MESH = pl.DeviceIdType.MESH
F32, BF16 = jnp.float32, jnp.bfloat16


def halves(value):
    high = value.astype(BF16)
    return high, (value - high.astype(F32)).astype(BF16)


def kernel(blocks, frags, *refs):
    virt = refs[0].shape[3]
    tall, flat = (2 * virt, 2 * virt), (virt, 2 * virt)

    def body(first, ladder, left, right):
        run(blocks, frags, first, ladder, left, right, *refs)

    pl.run_scoped(
        body,
        [[pltpu.ACC(m)(tall, F32) for _ in range(2)] for m in range(UNITS)],
        [[pltpu.ACC(m)(flat, F32) for _ in range(2)] for m in range(UNITS)],
        [pltpu.ACC(m)(flat, F32) for m in range(UNITS)],
        [pltpu.ACC(m)(flat, F32) for m in range(UNITS)],
    )


def run(
    blocks,
    frags,
    first_acc,
    ladder_acc,
    left_acc,
    right_acc,
    amps_hbm,
    exch_hbm,
    factors_hbm,
    hole_hbm,
    fock_hbm,
    orbital_hbm,
    pair_hbm,
    weight_hbm,
    export_hbm,
    new_ref,
    norm_ref,
    energy_ref,
    fact,
    amps_in,
    exch_in,
    fock_in,
    orbital_in,
    hole_ref,
    pair_ref,
    weight_ref,
    export_ref,
    amp,
    low,
    half,
    part,
    recv,
    base,
    recip,
    fock_row,
    fock_col,
    row_energy,
    row_t,
    sent_rows,
    got_rows,
    sums,
    in_sem,
    fact_sem,
    ag_send,
    ag_recv,
    rs_send,
    rs_recv,
    ex_send,
    ex_recv,
    sum_send,
    sum_recv,
):
    me = lax.axis_index("blk")
    frag = lax.axis_index("frag")
    rows, pairs, virt = amps_in.shape
    aux = fact.shape[0]
    groups = aux // GROUP
    border = export_hbm.shape[2]
    devices = blocks * frags
    device = frag * blocks + me
    peers = [lax.rem(me + j, blocks) for j in range(1, blocks)]
    starts = sorted(
        range(0, pairs, CHUNK), key=lambda p: p < border or p + CHUNK > pairs - border
    )
    chunks = len(starts)
    core_chunks = sum(1 for p in starts if border <= p and p + CHUNK <= pairs - border)
    turns = PASSES * chunks
    count = turns * groups

    def place(turn):
        return turn // chunks, starts[turn % chunks]

    def other(j):
        there = lax.rem(device + j, devices)
        return {"frag": there // blocks, "blk": lax.rem(there, blocks)}

    loads = []
    for i, (src, dst) in enumerate(
        (
            (amps_hbm.at[0], amps_in),
            (fock_hbm.at[0], fock_in),
            (orbital_hbm, orbital_in),
            (pair_hbm, pair_ref),
            (hole_hbm, hole_ref),
            (exch_hbm.at[0], exch_in),
            (weight_hbm, weight_ref),
            (export_hbm, export_ref),
        )
    ):
        loads.append(pltpu.make_async_copy(src, dst, in_sem.at[i]))
    fact_loads = [
        pltpu.make_async_copy(
            factors_hbm.at[0, pl.ds(g * GROUP, GROUP)],
            fact.at[pl.ds(g * GROUP, GROUP)],
            fact_sem.at[g],
        )
        for g in range(groups)
    ]
    for copy in loads[:6]:
        copy.start()
    for copy in fact_loads:
        copy.start()
    for copy in loads[6:]:
        copy.start()

    barrier = pltpu.get_barrier_semaphore()

    def greet(j, carry):
        pl.semaphore_signal(barrier, inc=1, device_id=other(j), device_id_type=MESH)
        return carry

    lax.fori_loop(1, devices, greet, 0)

    for m in range(UNITS):
        for ref in first_acc[m] + ladder_acc[m] + [left_acc[m], right_acc[m]]:
            pltpu.matmul_pop(ref)

    loads[0].wait()
    for p in range(pairs):
        value = amps_in[:, p, :]
        amp[0, p] = value
        low[0, me, p] = value.astype(BF16)
    pl.semaphore_wait(barrier, devices - 1)

    pending = []

    def gather(turn):
        sweep, start = place(turn)
        copies = []
        for j, peer in enumerate(peers):
            where = low.at[sweep, me, pl.ds(start, CHUNK)]
            copy = pltpu.make_async_remote_copy(
                src_ref=where,
                dst_ref=where,
                send_sem=ag_send.at[turn, j],
                recv_sem=ag_recv.at[turn, j],
                device_id={"blk": peer},
                device_id_type=MESH,
            )
            copy.start()
            copies.append(copy)
        pending.extend(copies)
        return copies

    gathers = {turn: gather(turn) for turn in range(chunks)}

    def scatter(turn):
        copies = []
        for j, peer in enumerate(peers):
            copy = pltpu.make_async_remote_copy(
                src_ref=part.at[turn, peer],
                dst_ref=recv.at[turn, j],
                send_sem=rs_send.at[turn, j],
                recv_sem=rs_recv.at[turn, j],
                device_id={"blk": peer},
                device_id_type=MESH,
            )
            copy.start()
            copies.append(copy)
        pending.extend(copies)
        return copies

    offset = pl.multiple_of(me * rows, rows)
    for copy in loads[1:5]:
        copy.wait()
    column = lax.broadcasted_iota(jnp.int32, (virt, virt), 1)
    own = (column >= offset) & (column < offset + rows)
    high, middle = halves(fock_in[...])
    fock_row[:, :virt] = high
    fock_row[:, virt:] = middle
    high, middle = halves(jnp.where(own, fock_in[...], 0.0))
    fock_col[:, :virt] = high
    fock_col[:, virt:] = middle
    row_t[...] = jnp.broadcast_to(orbital_in[...], (virt, virt)).T
    row_energy[...] = row_t[pl.ds(offset, rows), :] + orbital_in[...]
    for p in range(pairs):
        recip[p] = 1.0 / (row_energy[...] - pair_ref[0, p])
    loads[5].wait()

    def make_base(sweep, register):
        share = pairs // UNITS
        tile = jnp.concatenate([fock_row[...], jnp.zeros((virt, 2 * virt), BF16)], axis=0)
        for m in range(UNITS):
            pltpu.matmul_push_rhs(tile, staging_register=register, mxu_index=m, transpose=True)
        for m in range(UNITS):
            split = halves(amp[sweep, m * share : (m + 1) * share].reshape(share * rows, virt))
            for i, value in enumerate(split):
                pltpu.matmul_acc_lhs(
                    right_acc[m],
                    jnp.concatenate([value, value], axis=1),
                    load_staged_rhs=register if i == 0 else None,
                )
        for m in range(UNITS):
            product = pltpu.matmul_pop(right_acc[m])
            for k in range(share):
                p = m * share + k
                total = exch_in[:, p, :] + product[k * rows : (k + 1) * rows, :virt]
                for r in range(pairs):
                    total = total + hole_ref[0, p, r] * amp[sweep, r]
                total = total - (row_energy[...] - pair_ref[0, p]) * amp[sweep, p]
                base[sweep, p] = total

    make_base(0, 0)

    def add_left(turn, register):
        sweep, start = place(turn)
        split = [halves(amp[sweep, start + i]) for i in range(CHUNK)]
        for m in range(UNITS):
            tile = jnp.concatenate([split[i][m] for i in range(CHUNK)], axis=1)
            tile = jnp.concatenate([tile] * (2 * blocks), axis=0)
            pltpu.matmul_push_rhs(tile, staging_register=register, mxu_index=m)
            pltpu.matmul_acc_lhs(left_acc[m], fock_col[...], load_staged_rhs=register)

    def aux_at(step, m, i):
        return (step % groups) * GROUP + m * (GROUP // UNITS) + 2 * i

    def push_amp(step, register):
        turn = step // groups
        sweep, start = place(turn)
        if step % groups == 0:
            for copy in gathers[turn]:
                copy.wait_recv()
        tile = jnp.concatenate(
            [low[sweep, :, start + i].reshape(virt, virt) for i in range(CHUNK)], axis=1
        )
        tile = jnp.concatenate([tile, jnp.zeros((virt, 2 * virt), BF16)], axis=0)
        for m in range(UNITS):
            pltpu.matmul_push_rhs(tile, staging_register=register, mxu_index=m)

    def first_half(step, i, register):
        if step < groups and i == 0:
            fact_loads[step].wait()
        for m in range(UNITS):
            q = aux_at(step, m, i)
            slab = fact[q : q + 2].reshape(2 * virt, virt)
            pltpu.matmul_acc_lhs(
                first_acc[m][i],
                jnp.concatenate([slab, jnp.zeros_like(slab)], axis=1),
                load_staged_rhs=register if i == 0 else None,
            )

    def turn_half(i, register):
        for m in range(UNITS):
            done = pltpu.matmul_pop(first_acc[m][i]).astype(BF16)
            for p in range(CHUNK):
                for q in range(2):
                    half[m, i, p, q] = done[q * virt : (q + 1) * virt, p * virt : (p + 1) * virt]

    def push_half(i, register):
        for m in range(UNITS):
            tile = jnp.concatenate(
                [
                    jnp.concatenate([half[m, i, p, q] for q in range(2)], axis=1)
                    for p in range(CHUNK)
                ],
                axis=0,
            )
            pltpu.matmul_push_rhs(tile, staging_register=register, mxu_index=m, transpose=True)

    def second_half(step, i, register):
        turn = step // groups
        for m in range(UNITS):
            q = aux_at(step, m, i)
            pltpu.matmul_acc_lhs(
                ladder_acc[m][turn % 2],
                jnp.concatenate([fact[q], fact[q + 1]], axis=1),
                load_staged_rhs=register,
            )

    def group(step):
        now, free = step % 2, 1 - step % 2
        more = step + 1 < count
        turn_half(0, free)
        if more:
            first_half(step + 1, 0, now)
        push_half(0, free)
        turn_half(1, now)
        if more:
            first_half(step + 1, 1, now)
        push_half(1, now)
        second_half(step, 0, free)
        if step + 2 < count:
            push_amp(step + 2, free)
        second_half(step, 1, now)

    def give(turn):
        total = pltpu.matmul_pop(ladder_acc[0][turn % 2])
        side = pltpu.matmul_pop(left_acc[0])
        for m in range(1, UNITS):
            total = total + pltpu.matmul_pop(ladder_acc[m][turn % 2])
            side = side + pltpu.matmul_pop(left_acc[m])
        for i in range(CHUNK):
            cols = slice(i * virt, (i + 1) * virt)
            value = total[:, cols].T + side[:, cols]
            for k in range(blocks):
                part[turn, k, i] = value[k * rows : (k + 1) * rows]
        return scatter(turn)

    norm_sums = [jnp.zeros((8, virt), F32) for _ in range(PASSES)]

    def finish(turn, copies):
        sweep, start = place(turn)
        for copy in copies:
            copy.wait_recv()
        for i in range(CHUNK):
            p = start + i
            residual = base[sweep, p] + part[turn, me, i]
            for j in range(blocks - 1):
                residual = residual + recv[turn, j, i]
            norm_sums[sweep] += jnp.sum((residual * residual).reshape(rows // 8, 8, virt), axis=0)
            value = amp[sweep, p] + residual * recip[p]
            amp[sweep + 1, p] = value
            if sweep + 1 < PASSES:
                low[sweep + 1, me, p] = value.astype(BF16)
        if sweep + 1 < PASSES:
            gathers[turn + chunks] = gather(turn + chunks)

    exports = []

    def export():
        for side, target in ((0, lax.rem(frag + 1, frags)), (1, lax.rem(frag + frags - 1, frags))):
            for r in range(border):
                sent_rows[side, r] = amp[PASSES, export_ref[0, side, r]]
            copy = pltpu.make_async_remote_copy(
                src_ref=sent_rows.at[side],
                dst_ref=got_rows.at[side],
                send_sem=ex_send.at[side],
                recv_sem=ex_recv.at[side],
                device_id={"frag": target},
                device_id_type=MESH,
            )
            copy.start()
            exports.append(copy)
        pending.extend(exports)

    energy = [jnp.zeros((8, virt), F32)]

    def settle(p):
        value = amp[PASSES, p]
        if p < border:
            value = jnp.where(frag > 0, got_rows[0, p], value)
        if p >= pairs - border:
            value = jnp.where(frag < frags - 1, got_rows[1, p - (pairs - border)], value)
        new_ref[0, :, p, :] = value
        product = jnp.sum((value * exch_in[:, p, :]).reshape(rows // 8, 8, virt), axis=0)
        energy[0] = energy[0] + (weight_ref[0, p].astype(F32) * 0.5) * product

    push_amp(0, 1)
    first_half(0, 0, 1)
    first_half(0, 1, 1)
    push_amp(1, 0)
    given = {}
    for turn in range(turns):
        for g in range(groups):
            step = turn * groups + g
            group(step)
            if g == 0:
                if turn > 0:
                    given[turn - 1] = give(turn - 1)
                add_left(turn, step % 2)
            if g == groups // 2 - 1 and turn >= 2:
                finish(turn - 2, given[turn - 2])
                if turn - 2 == chunks - 1:
                    make_base(1, step % 2)
                if turn - 2 == (PASSES - 1) * chunks + core_chunks - 1:
                    for copy in loads[6:]:
                        copy.wait()
                    export()
    given[turns - 1] = give(turns - 1)
    finish(turns - 2, given[turns - 2])
    late = [p for t in range(turns - 1, turns) for p in range(place(t)[1], place(t)[1] + CHUNK)]
    for copy in exports:
        copy.wait_recv()
    for p in range(pairs):
        if p not in late:
            settle(p)
    finish(turns - 1, given[turns - 1])
    for p in late:
        settle(p)

    def whole(value):
        return jnp.sum(jnp.sum(value, axis=0, keepdims=True), axis=1, keepdims=True)

    lane = lax.broadcasted_iota(jnp.int32, (1, virt), 1)
    line = jnp.where(lane == PASSES, whole(energy[0]), 0.0)
    for s in range(PASSES):
        line = jnp.where(lane == s, whole(norm_sums[s]), line)
    sums[device] = line

    def sum_copy(j):
        return pltpu.make_async_remote_copy(
            src_ref=sums.at[device],
            dst_ref=sums.at[device],
            send_sem=sum_send.at[j - 1],
            recv_sem=sum_recv.at[j - 1],
            device_id=other(j),
            device_id_type=MESH,
        )

    def send_sum(j, carry):
        sum_copy(j).start()
        return carry

    def take_sum(j, carry):
        sum_copy(j).wait_recv()
        return carry

    def sent_sum(j, carry):
        sum_copy(j).wait_send()
        return carry

    lax.fori_loop(1, devices, send_sum, 0)
    for copy in pending:
        copy.wait_send()
    lax.fori_loop(1, devices, take_sum, 0)
    norm_ref[...] = jnp.sqrt(jnp.sum(sums[pl.ds(frag * blocks, blocks)], axis=0))[:, :PASSES]
    last = jnp.where(lane == PASSES, jnp.sum(sums[...], axis=0), 0.0)
    energy_ref[...] = -jnp.sum(last, axis=1, keepdims=True) / (virt * virt)
    lax.fori_loop(1, devices, sent_sum, 0)


def on_device(blocks, frags, *args):
    amps, _, factors = args[:3]
    _, rows, pairs, virt = amps.shape
    aux = factors.shape[1]
    border = args[-1].shape[2]
    turns = PASSES * (pairs // CHUNK)
    vmem = pl.BlockSpec(memory_space=pltpu.VMEM)
    hbm = pl.BlockSpec(memory_space=pltpu.HBM)
    dma = pltpu.SemaphoreType.DMA
    new_amps, norms, energy = pl.pallas_call(
        functools.partial(kernel, blocks, frags),
        out_shape=(
            jax.ShapeDtypeStruct(amps.shape, F32),
            jax.ShapeDtypeStruct((1, PASSES), F32),
            jax.ShapeDtypeStruct((1, 1), F32),
        ),
        in_specs=[hbm] * 9,
        out_specs=(vmem, vmem, vmem),
        scratch_shapes=[
            pltpu.VMEM((aux, virt, virt), BF16),
            pltpu.VMEM((rows, pairs, virt), F32),
            pltpu.VMEM((rows, pairs, virt), F32),
            pltpu.VMEM((virt, virt), F32),
            pltpu.VMEM((1, virt), F32),
            pltpu.SMEM((1, pairs, pairs), F32),
            pltpu.SMEM((1, pairs), F32),
            pltpu.SMEM((1, pairs), jnp.int32),
            pltpu.SMEM((1, 2, border), jnp.int32),
            pltpu.VMEM((PASSES + 1, pairs, rows, virt), F32),
            pltpu.VMEM((PASSES, blocks, pairs, rows, virt), BF16),
            pltpu.VMEM((UNITS, 2, CHUNK, 2, virt, virt), BF16),
            pltpu.VMEM((turns, blocks, CHUNK, rows, virt), F32),
            pltpu.VMEM((turns, blocks - 1, CHUNK, rows, virt), F32),
            pltpu.VMEM((PASSES, pairs, rows, virt), F32),
            pltpu.VMEM((pairs, rows, virt), F32),
            pltpu.VMEM((virt, 2 * virt), BF16),
            pltpu.VMEM((virt, 2 * virt), BF16),
            pltpu.VMEM((rows, virt), F32),
            pltpu.VMEM((virt, virt), F32),
            pltpu.VMEM((2, border, rows, virt), F32),
            pltpu.VMEM((2, border, rows, virt), F32),
            pltpu.VMEM((blocks * frags, 1, virt), F32),
            dma((8,)),
            dma((aux // GROUP,)),
            dma((turns, blocks - 1)),
            dma((turns, blocks - 1)),
            dma((turns, blocks - 1)),
            dma((turns, blocks - 1)),
            dma((2,)),
            dma((2,)),
            dma((blocks * frags - 1,)),
            dma((blocks * frags - 1,)),
        ],
        compiler_params=pltpu.CompilerParams(
            collective_id=0, has_side_effects=True, vmem_limit_bytes=48 * 2**20
        ),
    )(*[pltpu.with_memory_space_constraint(x, pltpu.HBM) for x in args])
    return new_amps, norms, energy.reshape(())


def solution(mesh):
    placed = (
        P("frag", "blk", None, None),
        P("frag", "blk", None, None),
        P("frag", "blk", None, None),
        P("frag", None, None),
        P("frag", None, None),
        P("frag", None),
        P("frag", None),
        P("frag", None),
        P("frag", None, None),
    )
    return jax.shard_map(
        functools.partial(on_device, mesh.shape["blk"], mesh.shape["frag"]),
        mesh=mesh,
        in_specs=placed,
        out_specs=(P("frag", "blk", None, None), P("frag", None), P()),
        check_vma=False,
    )
```

time: 73.7 us -> 46.4 us (0.63)
  Pallas kernels: 62 us -> 42.7 us
  local copies, waits for them, and re-layouts: 9.03 us -> 1.17 us
    pallas_call x1, Pallas kernels: 62 us -> 42.7 us  [on_device(): pl.pallas_call(functools.partial(kernel, blocks, frags), out_shape=(jax.S...]
    unnamed x20 -> x2, local copies, waits for them, and re-layouts: 9.03 us -> 1.17 us
where the time goes in v1:
time: 46.4 us; the launch traced here: 46.2 us
  Pallas kernels  42.7 us (92%)
  between operations  2.33 us (5%)
  local copies, waits for them, and re-layouts  1.17 us (3%)
    pallas_call x1, Pallas kernels, on_device(): pl.pallas_call(functools.partial(kernel, blocks, frags), out_shape=(jax.S...  42.7 us
    unnamed x2, local copies, waits for them, and re-layouts  1.17 us

profile of v1, /device:TPU:0, one launch (start us, length us, event | category | flops | bytes accessed | tf_op | source)
XLA Modules:
  0.0 46.2 jit_solution(10059431858144466735)
XLA Ops:
  0.6 42.7 %shard_map.112 = (f32[1,32,8,128]{3,2,1,0:T(8,128)S(1)}, f32[1,2]{1,0:T(1,128)S(1)}, f32[1,1]{1,0:T(1,128)}) custom-call(f32[1,32,8,128]{3,2,1,0:T(8,128)} %refs_0_.1, f32[1,32,8,128]{3,2,1,0:T(8,128)} %refs_1_.1, bf16[1,96,128,128]{3,2,1,0:T(8,128)(2,1)} %refs_2_.1, f32[1,8,8]{2,1,0:T(8,128)} %refs_3_.1, f32[1,128,128]{2,1,0:T(8,128)} %refs_4_.1, ...), custom_call_target="tpu_custom_call" | custom-call | tf_op jit(solution)/shard_map/pallas_call | solution.py:470
  43.4 0.7 %copy.15 = f32[1,32,8,128]{3,2,1,0:T(8,128)} copy(f32[1,32,8,128]{3,2,1,0:T(8,128)S(1)} %get-tuple-element.12) | data formatting | bytes 262144
  44.0 0.5 %copy.16 = f32[1,2]{1,0:T(1,128)} copy(f32[1,2]{1,0:T(1,128)S(1)} %get-tuple-element.13) | data formatting | bytes 16

commit v2 on v1

--- a/solution.py
+++ b/solution.py
@@ -69,6 +69,9 @@
     half,
     part,
     recv,
+    part_low,
+    recv_low,
+    exch,
     base,
     recip,
     fock_row,
@@ -77,7 +80,11 @@
     row_t,
     sent_rows,
     got_rows,
+    sent_weights,
+    got_weights,
     sums,
+    squares,
+    ring,
     in_sem,
     fact_sem,
     ag_send,
@@ -86,8 +93,12 @@
     rs_recv,
     ex_send,
     ex_recv,
+    we_send,
+    we_recv,
     sum_send,
     sum_recv,
+    sq_send,
+    sq_recv,
 ):
     me = lax.axis_index("blk")
     frag = lax.axis_index("frag")
@@ -95,23 +106,38 @@
     aux = fact.shape[0]
     groups = aux // GROUP
     border = export_hbm.shape[2]
-    devices = blocks * frags
     device = frag * blocks + me
     peers = [lax.rem(me + j, blocks) for j in range(1, blocks)]
-    starts = sorted(
-        range(0, pairs, CHUNK), key=lambda p: p < border or p + CHUNK > pairs - border
-    )
-    chunks = len(starts)
-    core_chunks = sum(1 for p in starts if border <= p and p + CHUNK <= pairs - border)
+    core = pairs - 2 * border
+    swap = frag == frags - 1
+
+    def pair_at(place):
+        if place < core:
+            return border + place
+        at = (place - core) % border
+        lower, upper = at, pairs - border + at
+        if place - core < border:
+            return jnp.where(swap, upper, lower)
+        return jnp.where(swap, lower, upper)
+
+    def take(ref, place):
+        if place < core:
+            return ref[:, border + place, :]
+        at = (place - core) % border
+        lower, upper = ref[:, at, :], ref[:, pairs - border + at, :]
+        if place - core < border:
+            return jnp.where(swap, upper, lower)
+        return jnp.where(swap, lower, upper)
+
+    chunks = pairs // CHUNK
+    core_chunks = core // CHUNK
     turns = PASSES * chunks
     count = turns * groups
 
     def place(turn):
-        return turn // chunks, starts[turn % chunks]
-
-    def other(j):
-        there = lax.rem(device + j, devices)
-        return {"frag": there // blocks, "blk": lax.rem(there, blocks)}
+        return turn // chunks, turn % chunks * CHUNK
+
+    sides = [lax.rem(frag + frags - 1, frags), lax.rem(frag + 1, frags)]
 
     loads = []
     for i, (src, dst) in enumerate(
@@ -135,31 +161,45 @@
         )
         for g in range(groups)
     ]
-    for copy in loads[:6]:
+    for copy in loads:
         copy.start()
     for copy in fact_loads:
         copy.start()
-    for copy in loads[6:]:
-        copy.start()
 
     barrier = pltpu.get_barrier_semaphore()
 
-    def greet(j, carry):
-        pl.semaphore_signal(barrier, inc=1, device_id=other(j), device_id_type=MESH)
-        return carry
-
-    lax.fori_loop(1, devices, greet, 0)
+    for peer in peers:
+        pl.semaphore_signal(barrier, inc=1, device_id={"blk": peer}, device_id_type=MESH)
+    for side in sides:
+        pl.semaphore_signal(barrier, inc=1, device_id={"frag": side}, device_id_type=MESH)
+
+    rounds = frags // 2
+    every = pl.cdiv(rounds, PASSES * chunks - 2)
+
+    def ring_signal(r):
+        for i, side in enumerate(sides):
+            pl.semaphore_signal(
+                ring.at[r, i], inc=1, device_id={"frag": side}, device_id_type=MESH
+            )
+
+    def ring_wait(r):
+        for i in range(2):
+            pl.semaphore_wait(ring.at[r, i], 1)
 
     for m in range(UNITS):
         for ref in first_acc[m] + ladder_acc[m] + [left_acc[m], right_acc[m]]:
             pltpu.matmul_pop(ref)
 
     loads[0].wait()
-    for p in range(pairs):
-        value = amps_in[:, p, :]
-        amp[0, p] = value
-        low[0, me, p] = value.astype(BF16)
-    pl.semaphore_wait(barrier, devices - 1)
+
+    def enter(place):
+        value = take(amps_in, place)
+        amp[0, place] = value
+        low[0, me, place] = value.astype(BF16)
+
+    for place_at in range(CHUNK):
+        enter(place_at)
+    pl.semaphore_wait(barrier, blocks - 1 + 2)
 
     pending = []
 
@@ -181,14 +221,19 @@
         pending.extend(copies)
         return copies
 
-    gathers = {turn: gather(turn) for turn in range(chunks)}
+    gathers = {0: gather(0)}
+    for turn in range(1, chunks):
+        for i in range(CHUNK):
+            enter(turn * CHUNK + i)
+        gathers[turn] = gather(turn)
 
     def scatter(turn):
         copies = []
+        last = turn == turns - 1
         for j, peer in enumerate(peers):
             copy = pltpu.make_async_remote_copy(
-                src_ref=part.at[turn, peer],
-                dst_ref=recv.at[turn, j],
+                src_ref=part_low.at[peer] if last else part.at[turn, peer],
+                dst_ref=recv_low.at[j] if last else recv.at[turn, j],
                 send_sem=rs_send.at[turn, j],
                 recv_sem=rs_recv.at[turn, j],
                 device_id={"blk": peer},
@@ -212,9 +257,33 @@
     fock_col[:, virt:] = middle
     row_t[...] = jnp.broadcast_to(orbital_in[...], (virt, virt)).T
     row_energy[...] = row_t[pl.ds(offset, rows), :] + orbital_in[...]
+    where = [pair_at(p) for p in range(pairs)]
+    levels = [pair_ref[0, p] for p in where]
     for p in range(pairs):
-        recip[p] = 1.0 / (row_energy[...] - pair_ref[0, p])
-    loads[5].wait()
+        recip[p] = 1.0 / (row_energy[...] - levels[p])
+    for copy in loads[5:]:
+        copy.wait()
+    weights = [weight_ref[0, p].astype(F32) * 0.5 for p in range(pairs)]
+    for p in range(pairs):
+        exch[p] = take(exch_in, p)
+    for i, side in enumerate(sides):
+        for r in range(border):
+            p = r if i == 0 else pairs - border + r
+            sent_weights[i, r] = exch_in[:, p, :] * weights[p]
+    weight_copies = []
+    for i, side in enumerate(sides):
+        copy = pltpu.make_async_remote_copy(
+            src_ref=sent_weights.at[i],
+            dst_ref=got_weights.at[i],
+            send_sem=we_send.at[i],
+            recv_sem=we_recv.at[i],
+            device_id={"frag": side},
+            device_id_type=MESH,
+        )
+        copy.start()
+        weight_copies.append(copy)
+    pending.extend(weight_copies)
+    ring_signal(0)
 
     def make_base(sweep, register):
         share = pairs // UNITS
@@ -233,10 +302,10 @@
             product = pltpu.matmul_pop(right_acc[m])
             for k in range(share):
                 p = m * share + k
-                total = exch_in[:, p, :] + product[k * rows : (k + 1) * rows, :virt]
+                total = exch[p] + product[k * rows : (k + 1) * rows, :virt]
                 for r in range(pairs):
-                    total = total + hole_ref[0, p, r] * amp[sweep, r]
-                total = total - (row_energy[...] - pair_ref[0, p]) * amp[sweep, p]
+                    total = total + hole_ref[0, where[p], where[r]] * amp[sweep, r]
+                total = total - (row_energy[...] - levels[p]) * amp[sweep, p]
                 base[sweep, p] = total
 
     make_base(0, 0)
@@ -332,34 +401,52 @@
             cols = slice(i * virt, (i + 1) * virt)
             value = total[:, cols].T + side[:, cols]
             for k in range(blocks):
-                part[turn, k, i] = value[k * rows : (k + 1) * rows]
+                piece = value[k * rows : (k + 1) * rows]
+                part[turn, k, i] = piece
+                if turn == turns - 1:
+                    part_low[k, i] = piece.astype(BF16)
         return scatter(turn)
 
     norm_sums = [jnp.zeros((8, virt), F32) for _ in range(PASSES)]
+    energy = [jnp.zeros((8, virt), F32)]
+
+    def fold(value):
+        return jnp.sum(value.reshape(rows // 8, 8, virt), axis=0)
 
     def finish(turn, copies):
         sweep, start = place(turn)
+        last = turn == turns - 1
         for copy in copies:
             copy.wait_recv()
         for i in range(CHUNK):
             p = start + i
             residual = base[sweep, p] + part[turn, me, i]
             for j in range(blocks - 1):
-                residual = residual + recv[turn, j, i]
-            norm_sums[sweep] += jnp.sum((residual * residual).reshape(rows // 8, 8, virt), axis=0)
+                residual = residual + (recv_low[j, i].astype(F32) if last else recv[turn, j, i])
+            norm_sums[sweep] += fold(residual * residual)
+            if last:
+                continue
             value = amp[sweep, p] + residual * recip[p]
             amp[sweep + 1, p] = value
             if sweep + 1 < PASSES:
                 low[sweep + 1, me, p] = value.astype(BF16)
+            elif p < core:
+                new_ref[:, border + p, :] = value
+                energy[0] = energy[0] + weights[border + p] * fold(value * exch[p])
         if sweep + 1 < PASSES:
             gathers[turn + chunks] = gather(turn + chunks)
 
     exports = []
 
     def export():
-        for side, target in ((0, lax.rem(frag + 1, frags)), (1, lax.rem(frag + frags - 1, frags))):
+        for copy in weight_copies:
+            copy.wait_recv()
+        for side, target in ((0, sides[1]), (1, sides[0])):
+            used = frag < frags - 1 if side == 0 else frag > 0
             for r in range(border):
-                sent_rows[side, r] = amp[PASSES, export_ref[0, side, r]]
+                value = amp[PASSES, jnp.maximum(export_ref[0, side, r] - border, 0)]
+                sent_rows[side, r] = value
+                energy[0] = energy[0] + jnp.where(used, fold(value * got_weights[side, r]), 0.0)
             copy = pltpu.make_async_remote_copy(
                 src_ref=sent_rows.at[side],
                 dst_ref=got_rows.at[side],
@@ -371,18 +458,6 @@
             copy.start()
             exports.append(copy)
         pending.extend(exports)
-
-    energy = [jnp.zeros((8, virt), F32)]
-
-    def settle(p):
-        value = amp[PASSES, p]
-        if p < border:
-            value = jnp.where(frag > 0, got_rows[0, p], value)
-        if p >= pairs - border:
-            value = jnp.where(frag < frags - 1, got_rows[1, p - (pairs - border)], value)
-        new_ref[0, :, p, :] = value
-        product = jnp.sum((value * exch_in[:, p, :]).reshape(rows // 8, 8, virt), axis=0)
-        energy[0] = energy[0] + (weight_ref[0, p].astype(F32) * 0.5) * product
 
     push_amp(0, 1)
     first_half(0, 0, 1)
@@ -397,65 +472,87 @@
                 if turn > 0:
                     given[turn - 1] = give(turn - 1)
                 add_left(turn, step % 2)
+            if g == 1 and 0 < turn < turns - 1:
+                for r in range((turn - 1) * every, min(turn * every, rounds)):
+                    ring_wait(r)
+                    if r + 1 < rounds:
+                        ring_signal(r + 1)
             if g == groups // 2 - 1 and turn >= 2:
                 finish(turn - 2, given[turn - 2])
                 if turn - 2 == chunks - 1:
                     make_base(1, step % 2)
                 if turn - 2 == (PASSES - 1) * chunks + core_chunks - 1:
-                    for copy in loads[6:]:
-                        copy.wait()
                     export()
     given[turns - 1] = give(turns - 1)
     finish(turns - 2, given[turns - 2])
-    late = [p for t in range(turns - 1, turns) for p in range(place(t)[1], place(t)[1] + CHUNK)]
-    for copy in exports:
-        copy.wait_recv()
-    for p in range(pairs):
-        if p not in late:
-            settle(p)
-    finish(turns - 1, given[turns - 1])
-    for p in late:
-        settle(p)
+    ends = (frag == 0) | swap
+    for i in range(border):
+        scale = weight_ref[0, where[core + i]].astype(F32) * 0.5
+        product = scale * fold(amp[PASSES, core + i] * exch[core + i])
+        energy[0] = energy[0] + jnp.where(ends, product, 0.0)
 
     def whole(value):
         return jnp.sum(jnp.sum(value, axis=0, keepdims=True), axis=1, keepdims=True)
 
     lane = lax.broadcasted_iota(jnp.int32, (1, virt), 1)
-    line = jnp.where(lane == PASSES, whole(energy[0]), 0.0)
-    for s in range(PASSES):
-        line = jnp.where(lane == s, whole(norm_sums[s]), line)
-    sums[device] = line
-
-    def sum_copy(j):
+    sums[device] = jnp.where(lane == 0, whole(energy[0]), 0.0)
+    blk_at = [lax.rem(me + j, blocks) for j in range(blocks)]
+
+    def sum_copy(i, j):
         return pltpu.make_async_remote_copy(
             src_ref=sums.at[device],
             dst_ref=sums.at[device],
-            send_sem=sum_send.at[j - 1],
-            recv_sem=sum_recv.at[j - 1],
-            device_id=other(j),
+            send_sem=sum_send.at[i * blocks + j],
+            recv_sem=sum_recv.at[i * blocks + j],
+            device_id={"frag": lax.rem(frag + i, frags), "blk": blk_at[j]},
             device_id_type=MESH,
         )
 
-    def send_sum(j, carry):
-        sum_copy(j).start()
-        return carry
-
-    def take_sum(j, carry):
-        sum_copy(j).wait_recv()
-        return carry
-
-    def sent_sum(j, carry):
-        sum_copy(j).wait_send()
-        return carry
-
-    lax.fori_loop(1, devices, send_sum, 0)
+    def all_sums(act):
+        def some(i, carry):
+            for j in range(blocks):
+                act(sum_copy(i, j))
+            return carry
+
+        lax.fori_loop(1, frags, some, 0)
+        for j in range(1, blocks):
+            act(sum_copy(0, j))
+
+    all_sums(lambda copy: copy.start())
+    finish(turns - 1, given[turns - 1])
+    line = jnp.zeros((1, virt), F32)
+    for s in range(PASSES):
+        line = jnp.where(lane == s, whole(norm_sums[s]), line)
+    squares[me] = line
+    copies = []
+    for j, peer in enumerate(peers):
+        copy = pltpu.make_async_remote_copy(
+            src_ref=squares.at[me],
+            dst_ref=squares.at[me],
+            send_sem=sq_send.at[j],
+            recv_sem=sq_recv.at[j],
+            device_id={"blk": peer},
+            device_id_type=MESH,
+        )
+        copy.start()
+        copies.append(copy)
+    for copy in exports:
+        copy.wait_recv()
+    for i in range(border):
+        value = amp[PASSES, core + i]
+        new_ref[:, i, :] = jnp.where(frag > 0, got_rows[0, i], value)
+        new_ref[:, pairs - border + i, :] = jnp.where(swap, value, got_rows[1, i])
     for copy in pending:
         copy.wait_send()
-    lax.fori_loop(1, devices, take_sum, 0)
-    norm_ref[...] = jnp.sqrt(jnp.sum(sums[pl.ds(frag * blocks, blocks)], axis=0))[:, :PASSES]
-    last = jnp.where(lane == PASSES, jnp.sum(sums[...], axis=0), 0.0)
-    energy_ref[...] = -jnp.sum(last, axis=1, keepdims=True) / (virt * virt)
-    lax.fori_loop(1, devices, sent_sum, 0)
+    for copy in copies:
+        copy.wait_recv()
+    norm_ref[...] = jnp.sqrt(jnp.sum(squares[...], axis=0))[:, :PASSES]
+    all_sums(lambda copy: copy.wait_recv())
+    total = jnp.sum(sums[...], axis=0)
+    energy_ref[...] = -jnp.sum(total, axis=1, keepdims=True) / (virt * virt)
+    for copy in copies:
+        copy.wait_send()
+    all_sums(lambda copy: copy.wait_send())
 
 
 def on_device(blocks, frags, *args):
@@ -470,7 +567,7 @@
     new_amps, norms, energy = pl.pallas_call(
         functools.partial(kernel, blocks, frags),
         out_shape=(
-            jax.ShapeDtypeStruct(amps.shape, F32),
+            jax.ShapeDtypeStruct(amps.shape[1:], F32),
             jax.ShapeDtypeStruct((1, PASSES), F32),
             jax.ShapeDtypeStruct((1, 1), F32),
         ),
@@ -491,6 +588,9 @@
             pltpu.VMEM((UNITS, 2, CHUNK, 2, virt, virt), BF16),
             pltpu.VMEM((turns, blocks, CHUNK, rows, virt), F32),
             pltpu.VMEM((turns, blocks - 1, CHUNK, rows, virt), F32),
+            pltpu.VMEM((blocks, CHUNK, rows, virt), BF16),
+            pltpu.VMEM((blocks - 1, CHUNK, rows, virt), BF16),
+            pltpu.VMEM((pairs, rows, virt), F32),
             pltpu.VMEM((PASSES, pairs, rows, virt), F32),
             pltpu.VMEM((pairs, rows, virt), F32),
             pltpu.VMEM((virt, 2 * virt), BF16),
@@ -499,7 +599,11 @@
             pltpu.VMEM((virt, virt), F32),
             pltpu.VMEM((2, border, rows, virt), F32),
             pltpu.VMEM((2, border, rows, virt), F32),
+            pltpu.VMEM((2, border, rows, virt), F32),
+            pltpu.VMEM((2, border, rows, virt), F32),
             pltpu.VMEM((blocks * frags, 1, virt), F32),
+            pltpu.VMEM((blocks, 1, virt), F32),
+            pltpu.SemaphoreType.REGULAR((frags // 2, 2)),
             dma((8,)),
             dma((aux // GROUP,)),
             dma((turns, blocks - 1)),
@@ -508,14 +612,18 @@
             dma((turns, blocks - 1)),
             dma((2,)),
             dma((2,)),
-            dma((blocks * frags - 1,)),
-            dma((blocks * frags - 1,)),
+            dma((2,)),
+            dma((2,)),
+            dma((blocks * frags,)),
+            dma((blocks * frags,)),
+            dma((blocks - 1,)),
+            dma((blocks - 1,)),
         ],
         compiler_params=pltpu.CompilerParams(
             collective_id=0, has_side_effects=True, vmem_limit_bytes=48 * 2**20
         ),
     )(*[pltpu.with_memory_space_constraint(x, pltpu.HBM) for x in args])
-    return new_amps, norms, energy.reshape(())
+    return new_amps.reshape(amps.shape), norms, energy.reshape(())
 
 
 def solution(mesh):

time: 46.4 us -> 43.9 us (0.946)
  Pallas kernels: 42.7 us -> 40.3 us
    pallas_call x1, Pallas kernels: 42.7 us -> 40.3 us  [on_device(): pl.pallas_call(functools.partial(kernel, blocks, frags), out_shape=(jax.S...]
where the time goes in v2:
time: 43.9 us; the launch traced here: 43.8 us
  Pallas kernels  40.3 us (92%)
  between operations  2.33 us (5%)
  local copies, waits for them, and re-layouts  1.17 us (3%)
    pallas_call x1, Pallas kernels, on_device(): pl.pallas_call(functools.partial(kernel, blocks, frags), out_shape=(jax.S...  40.3 us
    unnamed x2, local copies, waits for them, and re-layouts  1.17 us

profile of v2, /device:TPU:0, one launch (start us, length us, event | category | flops | bytes accessed | tf_op | source)
XLA Modules:
  0.0 43.8 jit_solution(17352749724693479463)
XLA Ops:
  0.6 40.3 %shard_map.112 = (f32[32,8,128]{2,1,0:T(8,128)S(1)}, f32[1,2]{1,0:T(1,128)S(1)}, f32[1,1]{1,0:T(1,128)}) custom-call(f32[1,32,8,128]{3,2,1,0:T(8,128)} %refs_0_.1, f32[1,32,8,128]{3,2,1,0:T(8,128)} %refs_1_.1, bf16[1,96,128,128]{3,2,1,0:T(8,128)(2,1)} %refs_2_.1, f32[1,8,8]{2,1,0:T(8,128)} %refs_3_.1, f32[1,128,128]{2,1,0:T(8,128)} %refs_4_.1, ...), custom_call_target="tpu_custom_call" | custom-call | tf_op jit(solution)/shard_map/pallas_call | solution.py:567
  40.9 0.7 %copy.15 = f32[1,32,8,128]{3,2,1,0:T(8,128)} copy(f32[1,32,8,128]{3,2,1,0:T(8,128)S(1)} %bitcast.2) | data formatting | bytes 262144
  41.6 0.5 %copy.16 = f32[1,2]{1,0:T(1,128)} copy(f32[1,2]{1,0:T(1,128)S(1)} %get-tuple-element.13) | data formatting | bytes 16

commit v3 on v2

--- a/solution.py
+++ b/solution.py
@@ -11,6 +11,8 @@
 CHUNK = 2
 UNITS = 2
 GROUP = 8
+GIVE = 1
+FINISH = 6
 MESH = pl.DeviceIdType.MESH
 F32, BF16 = jnp.float32, jnp.bfloat16
 
@@ -53,8 +55,7 @@
     weight_hbm,
     export_hbm,
     new_ref,
-    norm_ref,
-    energy_ref,
+    line_ref,
     fact,
     amps_in,
     exch_in,
@@ -139,6 +140,16 @@
 
     sides = [lax.rem(frag + frags - 1, frags), lax.rem(frag + 1, frags)]
 
+    def joint(ref, send_sem, recv_sem):
+        return pltpu.make_async_remote_copy(
+            src_ref=ref,
+            dst_ref=ref,
+            send_sem=send_sem,
+            recv_sem=recv_sem,
+            device_id={"blk": peers[0]},
+            device_id_type=MESH,
+        )
+
     loads = []
     for i, (src, dst) in enumerate(
         (
@@ -153,18 +164,10 @@
         )
     ):
         loads.append(pltpu.make_async_copy(src, dst, in_sem.at[i]))
-    fact_loads = [
-        pltpu.make_async_copy(
-            factors_hbm.at[0, pl.ds(g * GROUP, GROUP)],
-            fact.at[pl.ds(g * GROUP, GROUP)],
-            fact_sem.at[g],
-        )
-        for g in range(groups)
-    ]
+    fact_load = pltpu.make_async_copy(factors_hbm.at[0], fact, fact_sem)
     for copy in loads:
         copy.start()
-    for copy in fact_loads:
-        copy.start()
+    fact_load.start()
 
     barrier = pltpu.get_barrier_semaphore()
 
@@ -174,17 +177,17 @@
         pl.semaphore_signal(barrier, inc=1, device_id={"frag": side}, device_id_type=MESH)
 
     rounds = frags // 2
-    every = pl.cdiv(rounds, PASSES * chunks - 2)
-
-    def ring_signal(r):
+    every = pl.cdiv(rounds, turns - 3)
+
+    def ring_signal():
         for i, side in enumerate(sides):
             pl.semaphore_signal(
-                ring.at[r, i], inc=1, device_id={"frag": side}, device_id_type=MESH
+                ring.at[i], inc=1, device_id={"frag": side}, device_id_type=MESH
             )
 
-    def ring_wait(r):
+    def ring_wait():
         for i in range(2):
-            pl.semaphore_wait(ring.at[r, i], 1)
+            pl.semaphore_wait(ring.at[i], 1)
 
     for m in range(UNITS):
         for ref in first_acc[m] + ladder_acc[m] + [left_acc[m], right_acc[m]]:
@@ -205,21 +208,19 @@
 
     def gather(turn):
         sweep, start = place(turn)
-        copies = []
-        for j, peer in enumerate(peers):
-            where = low.at[sweep, me, pl.ds(start, CHUNK)]
-            copy = pltpu.make_async_remote_copy(
+        where = low.at[sweep, me, pl.ds(start, CHUNK)]
+        for peer in peers:
+            pltpu.make_async_remote_copy(
                 src_ref=where,
                 dst_ref=where,
-                send_sem=ag_send.at[turn, j],
-                recv_sem=ag_recv.at[turn, j],
+                send_sem=ag_send.at[turn],
+                recv_sem=ag_recv.at[turn],
                 device_id={"blk": peer},
                 device_id_type=MESH,
-            )
-            copy.start()
-            copies.append(copy)
-        pending.extend(copies)
-        return copies
+            ).start()
+        span = low.at[sweep, pl.ds(0, blocks - 1), pl.ds(start, CHUNK)]
+        pending.append(joint(span, ag_send.at[turn], ag_recv.at[turn]))
+        return pending[-1]
 
     gathers = {0: gather(0)}
     for turn in range(1, chunks):
@@ -228,21 +229,19 @@
         gathers[turn] = gather(turn)
 
     def scatter(turn):
-        copies = []
         last = turn == turns - 1
+        source, target = (part_low, recv_low) if last else (part.at[turn], recv.at[turn])
         for j, peer in enumerate(peers):
-            copy = pltpu.make_async_remote_copy(
-                src_ref=part_low.at[peer] if last else part.at[turn, peer],
-                dst_ref=recv_low.at[j] if last else recv.at[turn, j],
-                send_sem=rs_send.at[turn, j],
-                recv_sem=rs_recv.at[turn, j],
+            pltpu.make_async_remote_copy(
+                src_ref=source.at[peer],
+                dst_ref=target.at[j],
+                send_sem=rs_send.at[turn],
+                recv_sem=rs_recv.at[turn],
                 device_id={"blk": peer},
                 device_id_type=MESH,
-            )
-            copy.start()
-            copies.append(copy)
-        pending.extend(copies)
-        return copies
+            ).start()
+        pending.append(joint(target, rs_send.at[turn], rs_recv.at[turn]))
+        return pending[-1]
 
     offset = pl.multiple_of(me * rows, rows)
     for copy in loads[1:5]:
@@ -270,20 +269,18 @@
         for r in range(border):
             p = r if i == 0 else pairs - border + r
             sent_weights[i, r] = exch_in[:, p, :] * weights[p]
-    weight_copies = []
     for i, side in enumerate(sides):
-        copy = pltpu.make_async_remote_copy(
+        pltpu.make_async_remote_copy(
             src_ref=sent_weights.at[i],
             dst_ref=got_weights.at[i],
-            send_sem=we_send.at[i],
-            recv_sem=we_recv.at[i],
+            send_sem=we_send,
+            recv_sem=we_recv,
             device_id={"frag": side},
             device_id_type=MESH,
-        )
-        copy.start()
-        weight_copies.append(copy)
-    pending.extend(weight_copies)
-    ring_signal(0)
+        ).start()
+    weight_copy = joint(got_weights, we_send, we_recv)
+    pending.append(weight_copy)
+    ring_signal()
 
     def make_base(sweep, register):
         share = pairs // UNITS
@@ -326,8 +323,7 @@
         turn = step // groups
         sweep, start = place(turn)
         if step % groups == 0:
-            for copy in gathers[turn]:
-                copy.wait_recv()
+            gathers[turn].wait_recv()
         tile = jnp.concatenate(
             [low[sweep, :, start + i].reshape(virt, virt) for i in range(CHUNK)], axis=1
         )
@@ -336,8 +332,8 @@
             pltpu.matmul_push_rhs(tile, staging_register=register, mxu_index=m)
 
     def first_half(step, i, register):
-        if step < groups and i == 0:
-            fact_loads[step].wait()
+        if step == 0 and i == 0:
+            fact_load.wait()
         for m in range(UNITS):
             q = aux_at(step, m, i)
             slab = fact[q : q + 2].reshape(2 * virt, virt)
@@ -413,11 +409,9 @@
     def fold(value):
         return jnp.sum(value.reshape(rows // 8, 8, virt), axis=0)
 
-    def finish(turn, copies):
+    def finish(turn):
         sweep, start = place(turn)
         last = turn == turns - 1
-        for copy in copies:
-            copy.wait_recv()
         for i in range(CHUNK):
             p = start + i
             residual = base[sweep, p] + part[turn, me, i]
@@ -439,24 +433,22 @@
     exports = []
 
     def export():
-        for copy in weight_copies:
-            copy.wait_recv()
+        weight_copy.wait_recv()
         for side, target in ((0, sides[1]), (1, sides[0])):
             used = frag < frags - 1 if side == 0 else frag > 0
             for r in range(border):
                 value = amp[PASSES, jnp.maximum(export_ref[0, side, r] - border, 0)]
                 sent_rows[side, r] = value
                 energy[0] = energy[0] + jnp.where(used, fold(value * got_weights[side, r]), 0.0)
-            copy = pltpu.make_async_remote_copy(
+            pltpu.make_async_remote_copy(
                 src_ref=sent_rows.at[side],
                 dst_ref=got_rows.at[side],
-                send_sem=ex_send.at[side],
-                recv_sem=ex_recv.at[side],
+                send_sem=ex_send,
+                recv_sem=ex_recv,
                 device_id={"frag": target},
                 device_id_type=MESH,
-            )
-            copy.start()
-            exports.append(copy)
+            ).start()
+        exports.append(joint(got_rows, ex_send, ex_recv))
         pending.extend(exports)
 
     push_amp(0, 1)
@@ -464,27 +456,32 @@
     first_half(0, 1, 1)
     push_amp(1, 0)
     given = {}
+    ring_turn = turns - 1 - pl.cdiv(rounds, every)
     for turn in range(turns):
         for g in range(groups):
             step = turn * groups + g
+            if g == FINISH and turn >= 2:
+                given[turn - 2].wait_recv()
             group(step)
-            if g == 0:
+            if g == GIVE:
                 if turn > 0:
                     given[turn - 1] = give(turn - 1)
+                if ring_turn <= turn < turns - 1:
+                    at = (turn - ring_turn) * every
+                    for r in range(at, min(at + every, rounds)):
+                        ring_wait()
+                        if r + 1 < rounds:
+                            ring_signal()
                 add_left(turn, step % 2)
-            if g == 1 and 0 < turn < turns - 1:
-                for r in range((turn - 1) * every, min(turn * every, rounds)):
-                    ring_wait(r)
-                    if r + 1 < rounds:
-                        ring_signal(r + 1)
-            if g == groups // 2 - 1 and turn >= 2:
-                finish(turn - 2, given[turn - 2])
+            if g == FINISH and turn >= 2:
+                finish(turn - 2)
                 if turn - 2 == chunks - 1:
                     make_base(1, step % 2)
                 if turn - 2 == (PASSES - 1) * chunks + core_chunks - 1:
                     export()
     given[turns - 1] = give(turns - 1)
-    finish(turns - 2, given[turns - 2])
+    given[turns - 2].wait_recv()
+    finish(turns - 2)
     ends = (frag == 0) | swap
     for i in range(border):
         scale = weight_ref[0, where[core + i]].astype(F32) * 0.5
@@ -498,44 +495,41 @@
     sums[device] = jnp.where(lane == 0, whole(energy[0]), 0.0)
     blk_at = [lax.rem(me + j, blocks) for j in range(blocks)]
 
-    def sum_copy(i, j):
-        return pltpu.make_async_remote_copy(
+    def send_sum(i, j):
+        pltpu.make_async_remote_copy(
             src_ref=sums.at[device],
             dst_ref=sums.at[device],
-            send_sem=sum_send.at[i * blocks + j],
-            recv_sem=sum_recv.at[i * blocks + j],
+            send_sem=sum_send,
+            recv_sem=sum_recv,
             device_id={"frag": lax.rem(frag + i, frags), "blk": blk_at[j]},
             device_id_type=MESH,
-        )
-
-    def all_sums(act):
-        def some(i, carry):
-            for j in range(blocks):
-                act(sum_copy(i, j))
-            return carry
-
-        lax.fori_loop(1, frags, some, 0)
-        for j in range(1, blocks):
-            act(sum_copy(0, j))
-
-    all_sums(lambda copy: copy.start())
-    finish(turns - 1, given[turns - 1])
+        ).start()
+
+    def send_sums(i, carry):
+        for j in range(blocks):
+            send_sum(i, j)
+        return carry
+
+    lax.fori_loop(1, frags, send_sums, 0)
+    for j in range(1, blocks):
+        send_sum(0, j)
+    sum_copy = joint(sums.at[pl.ds(0, blocks * frags - 1)], sum_send, sum_recv)
+    given[turns - 1].wait_recv()
+    finish(turns - 1)
     line = jnp.zeros((1, virt), F32)
     for s in range(PASSES):
         line = jnp.where(lane == s, whole(norm_sums[s]), line)
     squares[me] = line
-    copies = []
-    for j, peer in enumerate(peers):
-        copy = pltpu.make_async_remote_copy(
+    for peer in peers:
+        pltpu.make_async_remote_copy(
             src_ref=squares.at[me],
             dst_ref=squares.at[me],
-            send_sem=sq_send.at[j],
-            recv_sem=sq_recv.at[j],
+            send_sem=sq_send,
+            recv_sem=sq_recv,
             device_id={"blk": peer},
             device_id_type=MESH,
-        )
-        copy.start()
-        copies.append(copy)
+        ).start()
+    square_copy = joint(squares.at[pl.ds(0, blocks - 1)], sq_send, sq_recv)
     for copy in exports:
         copy.wait_recv()
     for i in range(border):
@@ -544,15 +538,29 @@
         new_ref[:, pairs - border + i, :] = jnp.where(swap, value, got_rows[1, i])
     for copy in pending:
         copy.wait_send()
+    sum_copy.wait_send()
+    square_copy.wait_recv()
+    roots = jnp.sqrt(jnp.sum(squares[...], axis=0))
+    sum_copy.wait_recv()
+    total = jnp.sum(sums[...], axis=0)
+    scaled = -jnp.sum(total, axis=1, keepdims=True) / (virt * virt)
+    line_ref[...] = jnp.where(lane == PASSES, scaled, roots)
+    square_copy.wait_send()
+
+
+def hand_out(new_ref, line_ref, new_out, norm_out, energy_out, norm, energy, sem):
+    first = pltpu.make_async_copy(new_ref, new_out, sem.at[0])
+    first.start()
+    norm[...] = line_ref[:, :PASSES]
+    energy[...] = line_ref[:, PASSES : PASSES + 1]
+    copies = [
+        pltpu.make_async_copy(norm, norm_out, sem.at[1]),
+        pltpu.make_async_copy(energy, energy_out, sem.at[2]),
+    ]
     for copy in copies:
-        copy.wait_recv()
-    norm_ref[...] = jnp.sqrt(jnp.sum(squares[...], axis=0))[:, :PASSES]
-    all_sums(lambda copy: copy.wait_recv())
-    total = jnp.sum(sums[...], axis=0)
-    energy_ref[...] = -jnp.sum(total, axis=1, keepdims=True) / (virt * virt)
-    for copy in copies:
-        copy.wait_send()
-    all_sums(lambda copy: copy.wait_send())
+        copy.start()
+    for copy in [first] + copies:
+        copy.wait()
 
 
 def on_device(blocks, frags, *args):
@@ -564,15 +572,14 @@
     vmem = pl.BlockSpec(memory_space=pltpu.VMEM)
     hbm = pl.BlockSpec(memory_space=pltpu.HBM)
     dma = pltpu.SemaphoreType.DMA
-    new_amps, norms, energy = pl.pallas_call(
+    new_amps, line = pl.pallas_call(
         functools.partial(kernel, blocks, frags),
         out_shape=(
             jax.ShapeDtypeStruct(amps.shape[1:], F32),
-            jax.ShapeDtypeStruct((1, PASSES), F32),
-            jax.ShapeDtypeStruct((1, 1), F32),
+            jax.ShapeDtypeStruct((1, virt), F32),
         ),
         in_specs=[hbm] * 9,
-        out_specs=(vmem, vmem, vmem),
+        out_specs=(vmem, vmem),
         scratch_shapes=[
             pltpu.VMEM((aux, virt, virt), BF16),
             pltpu.VMEM((rows, pairs, virt), F32),
@@ -603,26 +610,35 @@
             pltpu.VMEM((2, border, rows, virt), F32),
             pltpu.VMEM((blocks * frags, 1, virt), F32),
             pltpu.VMEM((blocks, 1, virt), F32),
-            pltpu.SemaphoreType.REGULAR((frags // 2, 2)),
+            pltpu.SemaphoreType.REGULAR((2,)),
             dma((8,)),
-            dma((aux // GROUP,)),
-            dma((turns, blocks - 1)),
-            dma((turns, blocks - 1)),
-            dma((turns, blocks - 1)),
-            dma((turns, blocks - 1)),
-            dma((2,)),
-            dma((2,)),
-            dma((2,)),
-            dma((2,)),
-            dma((blocks * frags,)),
-            dma((blocks * frags,)),
-            dma((blocks - 1,)),
-            dma((blocks - 1,)),
+            dma,
+            dma((turns,)),
+            dma((turns,)),
+            dma((turns,)),
+            dma((turns,)),
+            dma,
+            dma,
+            dma,
+            dma,
+            dma,
+            dma,
+            dma,
+            dma,
         ],
         compiler_params=pltpu.CompilerParams(
             collective_id=0, has_side_effects=True, vmem_limit_bytes=48 * 2**20
         ),
     )(*[pltpu.with_memory_space_constraint(x, pltpu.HBM) for x in args])
+    shapes = (new_amps.shape, (1, PASSES), (1, 1))
+    new_amps, norms, energy = pl.pallas_call(
+        hand_out,
+        out_shape=tuple(jax.ShapeDtypeStruct(shape, F32) for shape in shapes),
+        in_specs=[vmem] * 2,
+        out_specs=(pl.BlockSpec(memory_space=pl.ANY),) * 3,
+        scratch_shapes=[pltpu.VMEM(shape, F32) for shape in shapes[1:]] + [dma((3,))],
+        compiler_params=pltpu.CompilerParams(vmem_limit_bytes=2**20),
+    )(new_amps, line)
     return new_amps.reshape(amps.shape), norms, energy.reshape(())
 
 

time: 43.9 us -> 39.5 us (0.90)
  Pallas kernels: 40.3 us -> 38.6 us
  between operations: 2.33 us -> 0.8 us
  local copies, waits for them, and re-layouts: 1.17 us -> 0 us
    pallas_call x1, Pallas kernels: 40.3 us -> 37.9 us  [on_device(): pl.pallas_call(functools.partial(kernel, blocks, frags), out_shape=(jax.S...]
    unnamed x2 -> x0, local copies, waits for them, and re-layouts: 1.17 us -> none
    pallas_call x0 -> x1, Pallas kernels: none -> 0.69 us  [on_device(): pl.pallas_call(hand_out, out_shape=tuple((jax.ShapeDtypeStruct(shape, F32...]
where the time goes in v3:
time: 39.5 us; the launch traced here: 39.4 us
  Pallas kernels  38.6 us (98%)
  between operations  0.8 us (2%)
    pallas_call x1, Pallas kernels, on_device(): pl.pallas_call(functools.partial(kernel, blocks, frags), out_shape=(jax.S...  37.9 us

profile of v3, /device:TPU:0, one launch (start us, length us, event | category | flops | bytes accessed | tf_op | source)
XLA Modules:
  0.0 39.4 jit_solution(2924249435537842193)
XLA Ops:
  0.6 37.9 %shard_map.112 = (f32[32,8,128]{2,1,0:T(8,128)S(1)}, f32[1,128]{1,0:T(1,128)S(1)}) custom-call(f32[1,32,8,128]{3,2,1,0:T(8,128)} %refs_0_.1, f32[1,32,8,128]{3,2,1,0:T(8,128)} %refs_1_.1, bf16[1,96,128,128]{3,2,1,0:T(8,128)(2,1)} %refs_2_.1, f32[1,8,8]{2,1,0:T(8,128)} %refs_3_.1, f32[1,128,128]{2,1,0:T(8,128)} %refs_4_.1, f32[1,128]{1,0:T(1,128)} %refs_5_.1, ...), custom_call_target="tpu_custom_call" | custom-call | tf_op jit(solution)/shard_map/pallas_call | solution.py:575
  38.5 0.7 %shard_map.113 = (f32[32,8,128]{2,1,0:T(8,128)}, f32[1,2]{1,0:T(1,128)}, f32[1,1]{1,0:T(1,128)}) custom-call(f32[32,8,128]{2,1,0:T(8,128)S(1)} %get-tuple-element.8.new_ref, f32[1,128]{1,0:T(1,128)S(1)} %get-tuple-element.9.line_ref), custom_call_target="tpu_custom_call" | custom-call | tf_op jit(solution)/shard_map/pallas_call | solution.py:634
